TPU v7x, 32 devices: a whole 2x2x4 slice. The times are simulated.
32 devices in a mesh: head: 8 (over z, x), client: 4 (over y, core).
Axes of the slice: x: 2, y: 2, z: 4, core: 2. Of those that a mesh axis runs over, the one named last changes fastest.
Arguments:
- client_ids: int32 [32], replicated, may hold values from 0 to 127, as said below
- client_table: bfloat16 [128, 256], replicated, may hold values from -6 to 6
- in_weight: bfloat16 [256, 4096], P(None, 'client'), may hold values from -0.375 to 0.375
- in_bias: float32 [4096], P('client'), may hold values from -3 to 3
- head_weight: bfloat16 [4096, 131072], P('client', 'head'), may hold values from -0.09375 to 0.09375
- tokens: int32 [32, 256], P(('head', 'client')), may hold values from 0 to 255
- labels: int32 [32, 256], P(('head', 'client')), may hold values from 0 to 255
- byte_table: bfloat16 [256, 4096], P(None, 'client'), may hold values from -5.5 to 6.7
- out_table: bfloat16 [256, 4096], P(None, 'client'), may hold values from -5.625 to 5.625
Outputs:
- head_grad: bfloat16 [4096, 131072], P('client', 'head')
- in_grad: float32 [256, 4096], P(None, 'client')
- losses: float32 [32], P(('head', 'client'))
Inputs may be any that keep to these rules, and one draw needn't show every extreme that they name: `client_ids`: distinct population indices.
All inputs are finite; a program needn't handle non-finite values.
Results may differ from a plain program's by a relative error of at most 0.0085.
Values may be sent and summed in bfloat16 or wider, within the bound.
A program may use at most 128 MiB of HBM per device.

v0:
```python
import jax
import jax.numpy as jnp
from jax import lax
from jax.sharding import PartitionSpec as P

EPSILON = 1e-06
learn_rate = 0.1


def client_loss(factor_a, factor_b, inputs, label_row, out_table):
    depth = factor_a.shape[0]
    rank_size = factor_a.shape[1]
    normed_in = inputs * lax.rsqrt(jnp.mean(inputs * inputs, -1, keepdims=True) + EPSILON)
    low_rank = jnp.dot(normed_in, factor_a, precision=lax.Precision.HIGHEST)
    adapted = inputs + jnp.dot(low_rank, factor_b, precision=lax.Precision.HIGHEST) / jnp.sqrt(
        jnp.float32(depth * rank_size)
    )
    normed = (adapted * lax.rsqrt(jnp.mean(adapted * adapted, -1, keepdims=True) + EPSILON)).astype(
        jnp.bfloat16
    )
    logits = lax.dot_general(
        normed, out_table, (((1,), (1,)), ((), ())), preferred_element_type=jnp.float32
    )
    logits = logits * (4.0 / jnp.sqrt(jnp.float32(depth)))
    log_total = jax.nn.logsumexp(logits, -1)
    vocab_ids = lax.broadcasted_iota(jnp.int32, logits.shape, 1)
    picked = jnp.sum(jnp.where(vocab_ids == label_row[:, None], logits, 0.0), -1)
    return jnp.sum(log_total - picked)


def train_client(factor_row, token_row, label_row, byte_table, out_table):
    depth = byte_table.shape[1]
    split_at = factor_row.shape[0] // 2
    rank_size = split_at // depth
    start_a = factor_row[:split_at].reshape(depth, rank_size).astype(jnp.float32)
    start_b = factor_row[split_at:].reshape(rank_size, depth).astype(jnp.float32)
    onehot = (
        token_row[:, None]
        == lax.broadcasted_iota(jnp.int32, (token_row.shape[0], byte_table.shape[0]), 1)
    ).astype(jnp.bfloat16)
    inputs = jnp.dot(onehot, byte_table, preferred_element_type=jnp.float32)
    loss_grad = jax.value_and_grad(client_loss, argnums=(0, 1))
    first_loss, (grad_a, grad_b) = loss_grad(start_a, start_b, inputs, label_row, out_table)
    middle_a = start_a - learn_rate * grad_a
    middle_b = start_b - learn_rate * grad_b
    second_loss, (grad_a, grad_b) = loss_grad(middle_a, middle_b, inputs, label_row, out_table)
    final_a = middle_a - learn_rate * grad_a
    final_b = middle_b - learn_rate * grad_b
    deltas = jnp.concatenate(
        [(final_a - start_a).reshape(-1), (final_b - start_b).reshape(-1)]
    ).astype(jnp.bfloat16)
    return (deltas, first_loss / token_row.shape[0])


def local(
    client_ids, client_table, in_weight, in_bias, head_weight, tokens, labels, byte_table, out_table
):
    head_count = lax.axis_size("head")
    group_count = lax.axis_size("client")
    per_device = tokens.shape[0]
    byte_full, out_full = (
        lax.all_gather(byte_table, "client", axis=1, tiled=True),
        lax.all_gather(out_table, "client", axis=1, tiled=True),
    )
    ordered = client_ids.reshape(head_count, group_count, per_device).transpose(1, 0, 2).reshape(-1)
    chosen = client_table[ordered]
    preact = jnp.dot(chosen, in_weight, preferred_element_type=jnp.float32) + in_bias
    hidden = jnp.maximum(preact, 0.0).astype(jnp.bfloat16)
    hidden_rows = hidden
    summed = lax.psum_scatter(
        jnp.dot(hidden_rows, head_weight, preferred_element_type=jnp.float32),
        "client",
        scatter_dimension=0,
        tiled=True,
    )
    owned = lax.all_to_all(
        summed.astype(jnp.bfloat16), "head", split_axis=0, concat_axis=1, tiled=True
    )

    def run_client(record):
        return train_client(record[0], record[1], record[2], byte_full, out_full)

    deltas, losses = lax.map(run_client, (owned, tokens, labels))
    returned = lax.all_to_all(deltas, "head", split_axis=1, concat_axis=0, tiled=True)
    received = lax.all_gather(returned, "client", axis=0, tiled=True)
    hidden_rows = hidden
    grad_sum = lax.dot_general(
        hidden_rows, received, (((0,), (0,)), ((), ())), preferred_element_type=jnp.float32
    )
    partial_value = lax.dot_general(
        received, head_weight, (((1,), (1,)), ((), ())), preferred_element_type=jnp.float32
    )
    hidden_back = partial_value
    grad_sum, hidden_back = (grad_sum, hidden_back)
    hidden_back = lax.psum(hidden_back, "head")
    masked = jnp.where(preact > 0, hidden_back, 0.0)
    in_grad = lax.dot_general(
        chosen.astype(jnp.float32),
        masked,
        (((0,), (0,)), ((), ())),
        precision=lax.Precision.HIGHEST,
    )
    return (grad_sum.astype(jnp.bfloat16), in_grad, losses)


def solution(mesh):
    placed = (
        P(),
        P(),
        P(None, "client"),
        P("client"),
        P("client", "head"),
        P(("head", "client"), None),
        P(("head", "client"), None),
        P(None, "client"),
        P(None, "client"),
    )
    return jax.shard_map(
        local,
        mesh=mesh,
        in_specs=placed,
        out_specs=(P("client", "head"), P(None, "client"), P(("head", "client"))),
        check_vma=False,
    )
```

profile of v0, /device:TPU:0, one launch (start us, length us, event | category | flops | bytes accessed | tf_op | source)
XLA Modules:
  0.0 274.1 jit_solution(7337150185194927193)
XLA Ops:
  7.2 0.0 reduce-scatter.2.cloned.1.call-start
  7.2 0.8 reshape.166
  8.0 0.1 copy.22
  8.1 0.1 reshape.167
  8.2 1.5 gather_fusion
  9.7 0.9 convolution_add_fusion
  10.5 14.9 %fusion.59 = f32[32,16384]{1,0:T(8,128)} fusion(bf16[1024,16384]{1,0:T(8,128)(2,1)} %param.13, f32[32,1024]{1,0:T(8,128)S(1)} %convolution_add_fusion), kind=kOutput, calls=%fused_computation.91 | convolution fusion | flops 1073807360 | bytes 35782656 | tf_op jit(solution)/shard_map/dot_general | solution.py:71
  25.4 0.0 reduce-scatter.2.cloned.1.call-update
  25.4 0.0 all-gather.5.cloned.1.call-start
  25.5 0.7 all-gather.5.cloned.1.call-update
  26.2 0.0 all-gather.7.cloned.1.call-start
  26.2 0.7 all-gather.7.cloned.1.call-update
  26.9 32.6 %reduce-scatter.2.cloned.1.call-done = f32[8,16384]{1,0:T(8,128)} async-done(((f32[32,16384]{1,0:T(8,128)}), f32[8,16384]{1,0:T(8,128)}) %reduce-scatter.2.cloned.1.call-update) | async-done | bytes 524304 | tf_op jit(solution)/shard_map/reduce_scatter | solution.py:70
  59.5 1.1 convert_bitcast_fusion
  60.6 0.5 broadcast.217
  61.1 0.8 reduce.4
  61.9 0.9 reshape.181
  62.8 5.5 %all-to-all-start = ((bf16[8,2,8192]{2,1,0:T(2,128)(2,1)}), bf16[8,2,8192]{2,1,0:T(2,128)(2,1)S(1)}, u32[]{:S(2)}, u32[]{:S(2)}) async-start(bf16[8,2,8192]{2,1,0:T(2,128)(2,1)} %reshape.181), calls=%async_computation.1 | async-start | bytes 524288 | tf_op jit(solution)/shard_map/all_to_all | solution.py:76
  68.3 0.0 all-gather.9.cloned.1.call-start
  68.3 15.3 %all-gather.5.cloned.1.call-done = bf16[256,4096]{1,0:T(8,128)(2,1)} async-done(((bf16[256,1024]{1,0:T(8,128)(2,1)}), bf16[256,4096]{1,0:T(8,128)(2,1)}) %all-gather.5.cloned.1.call-update) | async-done | bytes 2097168 | tf_op jit(solution)/shard_map/all_gather | solution.py:62
  83.7 4.4 %multiply_reduce_fusion.2 = (f32[256]{0:T(256)S(1)}, f32[256,4096]{1,0:T(8,128)}) fusion(bf16[256,4096]{1,0:T(8,128)(2,1)} %all-gather.5.cloned.1.call-done, s32[256]{0:T(256)S(1)} %bitcast.43), kind=kOutput, calls=%fused_computation.34 | convolution fusion | flops 539033344 | bytes 6293504 | tf_op jit(solution)/shard_map/while/body/eval_jaxpr/dot_general | solution.py:41
  88.0 0.8 reshape.182
  88.8 1.2 slice_reduce_fusion
  90.0 0.8 reshape.168
  90.8 0.1 reshape.169
  90.9 0.3 copy.24
  91.2 5.0 %fusion.18 = f32[256,16]{0,1:T(8,128)S(1)} fusion(bf16[4096,16]{1,0:T(8,128)(2,1)S(1)} %reshape.168, f32[256,4096]{1,0:T(8,128)} %get-tuple-element.34, f32[256]{0:T(256)S(1)} %add_rsqrt_fusion), kind=kOutput, calls=%fused_computation.39 | convolution fusion | flops 202375168 | bytes 4342784 | tf_op jit(solution)/shard_map/while/body/eval_jaxpr/jvp()/dot_general | solution.py:14
  96.3 0.0 copy-done.2
  96.3 4.3 %multiply_reduce_fusion.1 = (f32[256]{0:T(256)S(1)}, f32[256,4096]{1,0:T(8,128)}) fusion(f32[256,4096]{1,0:T(8,128)S(1)} %copy-done.2, f32[256,16]{0,1:T(8,128)S(1)} %fusion.18, bf16[16,4096]{1,0:T(8,128)(2,1)S(1)} %reshape.169), kind=kOutput, calls=%fused_computation.33 | convolution fusion | flops 205520640 | bytes 8537088 | tf_op jit(solution)/shard_map/while/body/eval_jaxpr/jvp()/dot_general | solution.py:15
  100.6 7.2 %all-gather.7.cloned.1.call-done = bf16[256,4096]{1,0:T(8,128)(2,1)} async-done(((bf16[256,1024]{1,0:T(8,128)(2,1)}), bf16[256,4096]{1,0:T(8,128)(2,1)}) %all-gather.7.cloned.1.call-update) | async-done | bytes 2097168 | tf_op jit(solution)/shard_map/all_gather | solution.py:63
  107.8 3.9 %fusion.78 = (f32[256]{0:T(256)S(1)}, f32[256,256]{0,1:T(8,128)S(1)}) fusion(bf16[256,4096]{1,0:T(8,128)(2,1)} %all-gather.7.cloned.1.call-done, f32[256,4096]{1,0:T(8,128)} %get-tuple-element.36, f32[256]{0:T(256)S(1)} %fusion.60), kind=kOutput, calls=%fused_computation.118 | convolution fusion | flops 539098880 | bytes 6555648 | tf_op jit(solution)/shard_map/while/body/eval_jaxpr/jvp()/dot_general | solution.py:21
  111.7 0.1 select_reduce_fusion
  111.8 0.6 subtract_reduce_fusion
  112.4 0.1 copy-done.5
  112.5 0.9 fusion.10
  113.5 2.8 %fusion.76 = f32[256,16]{0,1:T(8,128)S(1)} fusion(bf16[16,4096]{1,0:T(8,128)(2,1)S(1)} %reshape.169, bf16[256,4096]{1,0:T(8,128)(2,1)S(1)} %get-tuple-element.40, f32[256,4096]{1,0:T(8,128)S(1)} %copy-done.4, f32[256]{0:T(256)S(1)} %multiply_multiply_fusion.1, f32[256]{0:T(256)S(1)} %fusion.60), kind=kOutput, calls=%fused_computation.117 | convolution fusion | flops 207618048 | bytes 6440960 | tf_op jit(solution)/shard_map/while/body/eval_jaxpr/transpose(jvp())/dot_general | solution.py:15
  116.3 0.0 copy-start.3
  116.3 3.1 %fusion.6 = f32[16,4096]{1,0:T(8,128)S(1)} fusion(f32[256,16]{0,1:T(8,128)S(1)} %fusion.18, bf16[16,4096]{1,0:T(8,128)(2,1)S(1)} %reshape.169, bf16[256,4096]{1,0:T(8,128)(2,1)S(1)} %get-tuple-element.40, f32[256,4096]{1,0:T(8,128)S(1)} %copy-done.4, f32[256]{0:T(256)S(1)} %multiply_multiply_fusion.1, f32[256]{0:T(256)S(1)} %fusion.60), kind=kOutput, calls=%fused_computation.21 | convolution fusion | flops 207814656 | bytes 6703104 | tf_op jit(solution)/shard_map/while/body/eval_jaxpr/transpose(jvp())/dot_general | solution.py:15
  119.4 2.5 fusion.7
  121.9 3.4 %fusion.15 = f32[256,16]{0,1:T(8,128)S(1)} fusion(f32[4096,16]{0,1:T(8,128)S(1)} %fusion.7, f32[256,4096]{1,0:T(8,128)S(1)} %copy-done.3, f32[256]{0:T(256)S(1)} %add_rsqrt_fusion), kind=kOutput, calls=%fused_computation.36 | convolution fusion | flops 202375168 | bytes 4473856 | tf_op jit(solution)/shard_map/while/body/eval_jaxpr/jvp()/dot_general | solution.py:14
  125.4 4.1 %multiply_reduce_fusion = (f32[256]{0:T(256)S(1)}, f32[256,4096]{1,0:T(8,128)S(1)}) fusion(f32[256,4096]{1,0:T(8,128)S(1)} %copy-done.3, f32[256,16]{0,1:T(8,128)S(1)} %fusion.15, f32[16,4096]{1,0:T(8,128)S(1)} %fusion.6), kind=kOutput, calls=%fused_computation.31 | convolution fusion | flops 205520640 | bytes 8668160 | tf_op jit(solution)/shard_map/while/body/eval_jaxpr/jvp()/dot_general | solution.py:15
  129.5 0.9 fusion.79
  130.4 0.1 fusion.41
  130.4 0.9 fusion.11
  131.4 4.2 %fusion.73 = f32[256,16]{0,1:T(8,128)S(1)} fusion(f32[16,4096]{1,0:T(8,128)S(1)} %fusion.6, bf16[256,4096]{1,0:T(8,128)(2,1)S(1)} %get-tuple-element.46, f32[256,4096]{1,0:T(8,128)S(1)} %get-tuple-element.42, f32[256]{0:T(256)S(1)} %multiply_multiply_fusion, f32[256]{0:T(256)S(1)} %fusion.61), kind=kOutput, calls=%fused_computation.116 | convolution fusion | flops 207618048 | bytes 6572032 | tf_op jit(solution)/shard_map/while/body/eval_jaxpr/transpose(jvp())/dot_general | solution.py:15
  135.6 2.9 %fusion.9 = bf16[16,4096]{1,0:T(8,128)(2,1)S(1)} fusion(f32[16,4096]{1,0:T(8,128)S(1)} %fusion.6, f32[256,16]{0,1:T(8,128)S(1)} %fusion.15, bf16[16,4096]{1,0:T(8,128)(2,1)S(1)} %reshape.169, bf16[256,4096]{1,0:T(8,128)(2,1)S(1)} %get-tuple-element.46, f32[256,4096]{1,0:T(8,128)S(1)} %get-tuple-element.42, f32[256]{0:T(256)S(1)} %multiply_multiply_fusion, ...), kind=kOutput, calls=%fused_computation.25 | convolution fusion | flops 207945728 | bytes 6834176 | tf_op jit(solution)/shard_map/while/body/eval_jaxpr/transpose(jvp())/dot_general | solution.py:15
  138.5 2.5 fusion.8
  141.0 0.5 copy.25
  141.5 1.2 concatenate.17
  142.7 0.2 concatenate.18
  142.9 0.1 pad_maximum_fusion
  143.0 0.4 copy.29
  143.4 2.2 reduce.5
  145.7 0.2 reshape.183
  145.8 14.9 %all_to_all.26 = bf16[8,2,8192]{2,1,0:T(2,128)(2,1)S(1)} all-to-all(bf16[8,2,8192]{2,1,0:T(2,128)(2,1)S(1)} %reshape.183), channel_id=1, replica_groups=mesh['head'=8,'client'=4] {'head'}, dimensions={0} | all-to-all | bytes 524288 | tf_op jit(solution)/shard_map/all_to_all | solution.py:84
  160.7 0.3 reshape.184
  161.0 1.0 copy.27
  162.0 0.0 all-reduce.2.cloned.1.call-start
  162.6 14.3 %all-gather.9.cloned.1.call-done = bf16[1,32,16384]{2,1,0:T(8,128)(2,1)} async-done(((bf16[1,8,16384]{2,1,0:T(8,128)(2,1)}), bf16[1,32,16384]{2,1,0:T(8,128)(2,1)}) %all-gather.9.cloned.1.call-update) | async-done | bytes 1048592 | tf_op jit(solution)/shard_map/all_gather | solution.py:85
  177.0 16.1 %fusion.30 = f32[32,1024]{1,0:T(8,128)} fusion(bf16[1024,16384]{1,0:T(8,128)(2,1)} %param.13, bf16[1,32,16384]{2,1,0:T(8,128)(2,1)} %all-gather.9.cloned.1.call-done), kind=kOutput, calls=%fused_computation.52 | convolution fusion | flops 1073741824 | bytes 34734080 | tf_op jit(solution)/shard_map/dot_general | solution.py:90
  193.0 0.0 all-reduce.2.cloned.1.call-update
  193.1 14.9 %convolution_convert_fusion = bf16[1024,16384]{1,0:T(8,128)(2,1)} fusion(bf16[1,32,16384]{2,1,0:T(8,128)(2,1)S(1)} %copy-done.6, f32[32,1024]{1,0:T(8,128)S(1)} %convolution_add_fusion), kind=kOutput, calls=%fused_computation.1 | convolution fusion | flops 1090584576 | bytes 34734080 | tf_op jit(solution)/shard_map/dot_general | solution.py:87
  207.9 55.7 %all-reduce.2.cloned.1.call-done = f32[32,1024]{1,0:T(8,128)} async-done(((f32[32,1024]{1,0:T(8,128)}), f32[32,1024]{1,0:T(8,128)}) %all-reduce.2.cloned.1.call-update) | async-done | bytes 131088 | tf_op jit(solution)/shard_map/psum | solution.py:95
  263.7 2.5 fusion.42
  (27 shorter events, 0.1 us)
Async XLA Ops:
  7.2 2.5 copy-start
  7.2 52.3 %reduce-scatter.2.cloned.1.call-start = ((), (), s32[]{:S(2)}) async-start(), calls=%async_computation.3 | async-start | bytes 2621440 | tf_op jit(solution)/shard_map/reduce_scatter | solution.py:70
  25.4 58.2 %copy-start.7 = (s32[1,256]{1,0:T(1,128)S(1)}, s32[1,256]{1,0:T(1,128)}, u32[]{:S(2)}) copy-start(s32[1,256]{1,0:T(1,128)} %param.14) | copy-start | bytes 3076
  25.4 58.2 %all-gather.5.cloned.1.call-start = ((), (), s32[]{:S(2)}) async-start(), calls=%async_computation.4 | async-start | bytes 2621440 | tf_op jit(solution)/shard_map/all_gather | solution.py:62
  26.2 81.6 %all-gather.7.cloned.1.call-start = ((), (), s32[]{:S(2)}) async-start(), calls=%async_computation.5 | async-start | bytes 2621440 | tf_op jit(solution)/shard_map/all_gather | solution.py:63
  62.8 25.2 %all-to-all-start = ((bf16[8,2,8192]{2,1,0:T(2,128)(2,1)}), bf16[8,2,8192]{2,1,0:T(2,128)(2,1)S(1)}, u32[]{:S(2)}, u32[]{:S(2)}) async-start(bf16[8,2,8192]{2,1,0:T(2,128)(2,1)} %reshape.181), calls=%async_computation.1 | async-start | bytes 524288 | tf_op jit(solution)/shard_map/all_to_all | solution.py:76
  68.3 108.7 %all-gather.9.cloned.1.call-start = ((), (), s32[]{:S(2)}) async-start(), calls=%async_computation.7 | async-start | bytes 1310720 | tf_op jit(solution)/shard_map/all_gather | solution.py:85
  91.2 5.1 %copy-start.2 = (f32[256,4096]{1,0:T(8,128)S(1)}, f32[256,4096]{1,0:T(8,128)}, u32[]{:S(2)}) copy-start(f32[256,4096]{1,0:T(8,128)} %get-tuple-element.34) | copy-start | bytes 12582916
  100.6 11.1 %copy-start.8 = (s32[1,256]{1,0:T(1,128)S(1)}, s32[1,256]{1,0:T(1,128)}, u32[]{:S(2)}) copy-start(s32[1,256]{1,0:T(1,128)} %param.15) | copy-start | bytes 3076
  107.8 4.6 %copy-start.4 = (f32[256,4096]{1,0:T(8,128)S(1)}, f32[256,4096]{1,0:T(8,128)}, u32[]{:S(2)}) copy-start(f32[256,4096]{1,0:T(8,128)} %get-tuple-element.36) | copy-start | bytes 12582916
  107.8 4.7 %copy-start.5 = (bf16[256,4096]{1,0:T(8,128)(2,1)S(1)}, bf16[256,4096]{1,0:T(8,128)(2,1)}, u32[]{:S(2)}) copy-start(bf16[256,4096]{1,0:T(8,128)(2,1)} %all-gather.7.cloned.1.call-done) | copy-start | bytes 6291460
  116.3 3.1 %copy-start.3 = (f32[256,4096]{1,0:T(8,128)S(1)}, f32[256,4096]{1,0:T(8,128)}, u32[]{:S(2)}) copy-start(f32[256,4096]{1,0:T(8,128)} %get-tuple-element.34) | copy-start | bytes 12582916
  162.0 101.7 %all-reduce.2.cloned.1.call-start = ((), (), s32[]{:S(2)}) async-start(), calls=%async_computation.6 | async-start | bytes 262144 | tf_op jit(solution)/shard_map/psum | solution.py:95
  177.0 16.1 %copy-start.6 = (bf16[1,32,16384]{2,1,0:T(8,128)(2,1)S(1)}, bf16[1,32,16384]{2,1,0:T(8,128)(2,1)}, u32[]{:S(2)}) copy-start(bf16[1,32,16384]{2,1,0:T(8,128)(2,1)} %all-gather.9.cloned.1.call-done) | copy-start | bytes 3145732
  193.1 73.1 %copy-start.1 = (bf16[256,1024]{1,0:T(8,128)(2,1)S(1)}, bf16[256,1024]{1,0:T(8,128)(2,1)}, u32[]{:S(2)}) copy-start(bf16[256,1024]{1,0:T(8,128)(2,1)} %param.11) | copy-start | bytes 1572868
Sparse Core Ops, SparseCore 0:
  25.6 33.9 reduce-scatter.1
  61.1 22.5 all-gather.4
  85.2 22.5 all-gather.6
  162.1 14.7 all-gather.8
  193.2 70.4 all-reduce.1
where the time goes:
time: 278 us; the launch traced here: 274 us
  waiting for transfers between devices  127 us (46%)
  matrix products  95 us (34%)
  between operations  15.9 us (6%)
  blocking collectives  14.9 us (5%)
  local copies, waits for them, and re-layouts  10.8 us (4%)
  starting transfers between devices  5.69 us (2%)
  other arithmetic  5.08 us (2%)
    psum x1, waiting for transfers between devices, local(): hidden_back = lax.psum(hidden_back, 'head')  55.7 us
    reduce_scatter x1, waiting for transfers between devices, local(): lax.psum_scatter(jnp.dot(hidden_rows, head_weight, preferred_element_type...  32.6 us
    dot_general x6, matrix products, client_loss(): jnp.dot(low_rank, factor_b, precision=lax.Precision.HIGHEST)  21.5 us
    dot_general x1, matrix products, local(): lax.dot_general(received, head_weight, (((1,), (1,)), ((), ())), preferre...  16.1 us
    all_gather x1, waiting for transfers between devices, local(): lax.all_gather(byte_table, 'client', axis=1, tiled=True)  15.3 us
    all_to_all x1, blocking collectives, local(): lax.all_to_all(deltas, 'head', split_axis=1, concat_axis=0, tiled=True)  14.9 us
    dot_general x1, matrix products, local(): lax.dot_general(hidden_rows, received, (((0,), (0,)), ((), ())), preferre...  14.9 us
    dot_general x1, matrix products, local(): jnp.dot(hidden_rows, head_weight, preferred_element_type=jnp.float32)  14.9 us
  transfers between devices with their start and end apart: 6, of which 5 were waited for; matrix products, arithmetic and copies ran while one was open for 13% of the time, Pallas kernels for 0%

commit v1 on v0

--- a/solution.py
+++ b/solution.py
@@ -92,7 +92,7 @@
     )
     hidden_back = partial_value
     grad_sum, hidden_back = (grad_sum, hidden_back)
-    hidden_back = lax.psum(hidden_back, "head")
+    hidden_back = lax.all_gather(hidden_back, "head").sum(axis=0)
     masked = jnp.where(preact > 0, hidden_back, 0.0)
     in_grad = lax.dot_general(
         chosen.astype(jnp.float32),

time: 278 us -> 248 us (0.89)
  waiting for transfers between devices: 127 us -> 96.4 us
    psum x1 -> x0, waiting for transfers between devices: 55.7 us -> none  [local(): hidden_back = lax.psum(hidden_back, 'head')]
    all_gather x0 -> x1, waiting for transfers between devices: none -> 24.9 us  [local(): hidden_back = lax.all_gather(hidden_back, 'head').sum(axis=0)]
  transfers between devices with their start and end apart: 6 -> 6, of which waited for: 5 -> 5; matrix products, arithmetic and copies ran while one was open for 13% -> 14% of each run, Pallas kernels for 0% -> 0%
where the time goes in v1:
time: 248 us; the launch traced here: 244 us
  waiting for transfers between devices  96.4 us (39%)
  matrix products  94.1 us (38%)
  between operations  16 us (6%)
  blocking collectives  14.9 us (6%)
  local copies, waits for them, and re-layouts  10.8 us (4%)
  other arithmetic  6.37 us (3%)
  starting transfers between devices  5.69 us (2%)
    reduce_scatter x1, waiting for transfers between devices, local(): lax.psum_scatter(jnp.dot(hidden_rows, head_weight, preferred_element_type...  32.6 us
    all_gather x1, waiting for transfers between devices, local(): hidden_back = lax.all_gather(hidden_back, 'head').sum(axis=0)  24.9 us
    dot_general x6, matrix products, client_loss(): jnp.dot(low_rank, factor_b, precision=lax.Precision.HIGHEST)  21.5 us
    dot_general x1, matrix products, local(): lax.dot_general(received, head_weight, (((1,), (1,)), ((), ())), preferre...  16.1 us
    all_gather x1, waiting for transfers between devices, local(): lax.all_gather(byte_table, 'client', axis=1, tiled=True)  15.3 us
    all_gather x1, waiting for transfers between devices, local(): received = lax.all_gather(returned, 'client', axis=0, tiled=True)  14.9 us
    all_to_all x1, blocking collectives, local(): lax.all_to_all(deltas, 'head', split_axis=1, concat_axis=0, tiled=True)  14.9 us
    dot_general x1, matrix products, local(): lax.dot_general(hidden_rows, received, (((0,), (0,)), ((), ())), preferre...  14.9 us
  transfers between devices with their start and end apart: 6, of which 5 were waited for; matrix products, arithmetic and copies ran while one was open for 14% of the time, Pallas kernels for 0%

profile of v1, /device:TPU:0, one launch (start us, length us, event | category | flops | bytes accessed | tf_op | source)
XLA Modules:
  0.0 244.3 jit_solution(1335589572747601965)
XLA Ops:
  7.2 0.0 reduce-scatter.2.cloned.1.call-start
  7.2 0.8 reshape.166
  8.0 0.1 copy.22
  8.1 0.1 reshape.167
  8.2 1.5 gather_fusion
  9.7 0.9 convolution_add_fusion
  10.5 14.9 %fusion.59 = f32[32,16384]{1,0:T(8,128)} fusion(bf16[1024,16384]{1,0:T(8,128)(2,1)} %param.13, f32[32,1024]{1,0:T(8,128)S(1)} %convolution_add_fusion), kind=kOutput, calls=%fused_computation.91 | convolution fusion | flops 1073807360 | bytes 35782656 | tf_op jit(solution)/shard_map/dot_general | solution.py:71
  25.4 0.0 reduce-scatter.2.cloned.1.call-update
  25.4 0.0 all-gather.7.cloned.1.call-start
  25.5 0.7 all-gather.7.cloned.1.call-update
  26.2 0.0 all-gather.9.cloned.1.call-start
  26.2 0.7 all-gather.9.cloned.1.call-update
  26.9 32.6 %reduce-scatter.2.cloned.1.call-done = f32[8,16384]{1,0:T(8,128)} async-done(((f32[32,16384]{1,0:T(8,128)}), f32[8,16384]{1,0:T(8,128)}) %reduce-scatter.2.cloned.1.call-update) | async-done | bytes 524304 | tf_op jit(solution)/shard_map/reduce_scatter | solution.py:70
  59.5 1.1 convert_bitcast_fusion
  60.6 0.5 broadcast.217
  61.1 0.8 reduce.4
  61.9 0.9 reshape.182
  62.8 5.5 %all-to-all-start = ((bf16[8,2,8192]{2,1,0:T(2,128)(2,1)}), bf16[8,2,8192]{2,1,0:T(2,128)(2,1)S(1)}, u32[]{:S(2)}, u32[]{:S(2)}) async-start(bf16[8,2,8192]{2,1,0:T(2,128)(2,1)} %reshape.182), calls=%async_computation.1 | async-start | bytes 524288 | tf_op jit(solution)/shard_map/all_to_all | solution.py:76
  68.3 0.0 all-gather.11.cloned.1.call-start
  68.3 15.3 %all-gather.7.cloned.1.call-done = bf16[256,4096]{1,0:T(8,128)(2,1)} async-done(((bf16[256,1024]{1,0:T(8,128)(2,1)}), bf16[256,4096]{1,0:T(8,128)(2,1)}) %all-gather.7.cloned.1.call-update) | async-done | bytes 2097168 | tf_op jit(solution)/shard_map/all_gather | solution.py:62
  83.7 4.4 %multiply_reduce_fusion.2 = (f32[256]{0:T(256)S(1)}, f32[256,4096]{1,0:T(8,128)}) fusion(bf16[256,4096]{1,0:T(8,128)(2,1)} %all-gather.7.cloned.1.call-done, s32[256]{0:T(256)S(1)} %bitcast.45), kind=kOutput, calls=%fused_computation.34 | convolution fusion | flops 539033344 | bytes 6293504 | tf_op jit(solution)/shard_map/while/body/eval_jaxpr/dot_general | solution.py:41
  88.0 0.8 reshape.183
  88.8 1.2 slice_reduce_fusion
  90.0 0.8 reshape.168
  90.8 0.1 reshape.169
  90.9 0.3 copy.24
  91.2 5.0 %fusion.18 = f32[256,16]{0,1:T(8,128)S(1)} fusion(bf16[4096,16]{1,0:T(8,128)(2,1)S(1)} %reshape.168, f32[256,4096]{1,0:T(8,128)} %get-tuple-element.34, f32[256]{0:T(256)S(1)} %add_rsqrt_fusion), kind=kOutput, calls=%fused_computation.39 | convolution fusion | flops 202375168 | bytes 4342784 | tf_op jit(solution)/shard_map/while/body/eval_jaxpr/jvp()/dot_general | solution.py:14
  96.3 0.0 copy-done.2
  96.3 4.3 %multiply_reduce_fusion.1 = (f32[256]{0:T(256)S(1)}, f32[256,4096]{1,0:T(8,128)}) fusion(f32[256,4096]{1,0:T(8,128)S(1)} %copy-done.2, f32[256,16]{0,1:T(8,128)S(1)} %fusion.18, bf16[16,4096]{1,0:T(8,128)(2,1)S(1)} %reshape.169), kind=kOutput, calls=%fused_computation.33 | convolution fusion | flops 205520640 | bytes 8537088 | tf_op jit(solution)/shard_map/while/body/eval_jaxpr/jvp()/dot_general | solution.py:15
  100.6 7.2 %all-gather.9.cloned.1.call-done = bf16[256,4096]{1,0:T(8,128)(2,1)} async-done(((bf16[256,1024]{1,0:T(8,128)(2,1)}), bf16[256,4096]{1,0:T(8,128)(2,1)}) %all-gather.9.cloned.1.call-update) | async-done | bytes 2097168 | tf_op jit(solution)/shard_map/all_gather | solution.py:63
  107.8 3.9 %fusion.78 = (f32[256]{0:T(256)S(1)}, f32[256,256]{0,1:T(8,128)S(1)}) fusion(bf16[256,4096]{1,0:T(8,128)(2,1)} %all-gather.9.cloned.1.call-done, f32[256,4096]{1,0:T(8,128)} %get-tuple-element.36, f32[256]{0:T(256)S(1)} %fusion.60), kind=kOutput, calls=%fused_computation.118 | convolution fusion | flops 539098880 | bytes 6555648 | tf_op jit(solution)/shard_map/while/body/eval_jaxpr/jvp()/dot_general | solution.py:21
  111.7 0.1 select_reduce_fusion
  111.8 0.6 subtract_reduce_fusion
  112.4 0.1 copy-done.5
  112.5 0.9 fusion.10
  113.5 2.8 %fusion.76 = f32[256,16]{0,1:T(8,128)S(1)} fusion(bf16[16,4096]{1,0:T(8,128)(2,1)S(1)} %reshape.169, bf16[256,4096]{1,0:T(8,128)(2,1)S(1)} %get-tuple-element.40, f32[256,4096]{1,0:T(8,128)S(1)} %copy-done.4, f32[256]{0:T(256)S(1)} %multiply_multiply_fusion.1, f32[256]{0:T(256)S(1)} %fusion.60), kind=kOutput, calls=%fused_computation.117 | convolution fusion | flops 207618048 | bytes 6440960 | tf_op jit(solution)/shard_map/while/body/eval_jaxpr/transpose(jvp())/dot_general | solution.py:15
  116.3 0.0 copy-start.3
  116.3 3.1 %fusion.6 = f32[16,4096]{1,0:T(8,128)S(1)} fusion(f32[256,16]{0,1:T(8,128)S(1)} %fusion.18, bf16[16,4096]{1,0:T(8,128)(2,1)S(1)} %reshape.169, bf16[256,4096]{1,0:T(8,128)(2,1)S(1)} %get-tuple-element.40, f32[256,4096]{1,0:T(8,128)S(1)} %copy-done.4, f32[256]{0:T(256)S(1)} %multiply_multiply_fusion.1, f32[256]{0:T(256)S(1)} %fusion.60), kind=kOutput, calls=%fused_computation.21 | convolution fusion | flops 207814656 | bytes 6703104 | tf_op jit(solution)/shard_map/while/body/eval_jaxpr/transpose(jvp())/dot_general | solution.py:15
  119.4 2.5 %fusion.7 = f32[4096,16]{0,1:T(8,128)S(1)} fusion(f32[256,16]{0,1:T(8,128)S(1)} %fusion.76, f32[256,4096]{1,0:T(8,128)S(1)} %copy-done.3, f32[256]{0:T(256)S(1)} %add_rsqrt_fusion, bf16[4096,16]{0,1:T(8,128)(2,1)S(1)} %copy.24), kind=kOutput, calls=%fused_computation.23 | convolution fusion | flops 202571776 | bytes 4604928 | tf_op jit(solution)/shard_map/while/body/eval_jaxpr/transpose(jvp())/dot_general | solution.py:14
  121.9 3.4 %fusion.15 = f32[256,16]{0,1:T(8,128)S(1)} fusion(f32[4096,16]{0,1:T(8,128)S(1)} %fusion.7, f32[256,4096]{1,0:T(8,128)S(1)} %copy-done.3, f32[256]{0:T(256)S(1)} %add_rsqrt_fusion), kind=kOutput, calls=%fused_computation.36 | convolution fusion | flops 202375168 | bytes 4473856 | tf_op jit(solution)/shard_map/while/body/eval_jaxpr/jvp()/dot_general | solution.py:14
  125.4 4.1 %multiply_reduce_fusion = (f32[256]{0:T(256)S(1)}, f32[256,4096]{1,0:T(8,128)S(1)}) fusion(f32[256,4096]{1,0:T(8,128)S(1)} %copy-done.3, f32[256,16]{0,1:T(8,128)S(1)} %fusion.15, f32[16,4096]{1,0:T(8,128)S(1)} %fusion.6), kind=kOutput, calls=%fused_computation.31 | convolution fusion | flops 205520640 | bytes 8668160 | tf_op jit(solution)/shard_map/while/body/eval_jaxpr/jvp()/dot_general | solution.py:15
  129.5 0.9 fusion.79
  130.4 0.1 fusion.41
  130.4 0.9 fusion.11
  131.4 4.2 %fusion.73 = f32[256,16]{0,1:T(8,128)S(1)} fusion(f32[16,4096]{1,0:T(8,128)S(1)} %fusion.6, bf16[256,4096]{1,0:T(8,128)(2,1)S(1)} %get-tuple-element.46, f32[256,4096]{1,0:T(8,128)S(1)} %get-tuple-element.42, f32[256]{0:T(256)S(1)} %multiply_multiply_fusion, f32[256]{0:T(256)S(1)} %fusion.61), kind=kOutput, calls=%fused_computation.116 | convolution fusion | flops 207618048 | bytes 6572032 | tf_op jit(solution)/shard_map/while/body/eval_jaxpr/transpose(jvp())/dot_general | solution.py:15
  135.6 2.9 %fusion.9 = bf16[16,4096]{1,0:T(8,128)(2,1)S(1)} fusion(f32[16,4096]{1,0:T(8,128)S(1)} %fusion.6, f32[256,16]{0,1:T(8,128)S(1)} %fusion.15, bf16[16,4096]{1,0:T(8,128)(2,1)S(1)} %reshape.169, bf16[256,4096]{1,0:T(8,128)(2,1)S(1)} %get-tuple-element.46, f32[256,4096]{1,0:T(8,128)S(1)} %get-tuple-element.42, f32[256]{0:T(256)S(1)} %multiply_multiply_fusion, ...), kind=kOutput, calls=%fused_computation.25 | convolution fusion | flops 207945728 | bytes 6834176 | tf_op jit(solution)/shard_map/while/body/eval_jaxpr/transpose(jvp())/dot_general | solution.py:15
  138.5 2.5 %fusion.8 = bf16[4096,16]{0,1:T(8,128)(2,1)S(1)} fusion(f32[4096,16]{0,1:T(8,128)S(1)} %fusion.7, f32[256,16]{0,1:T(8,128)S(1)} %fusion.73, f32[256,4096]{1,0:T(8,128)S(1)} %copy-done.3, f32[256]{0:T(256)S(1)} %add_rsqrt_fusion, bf16[4096,16]{0,1:T(8,128)(2,1)S(1)} %copy.24), kind=kOutput, calls=%fused_computation.24 | convolution fusion | flops 202702848 | bytes 4736000 | tf_op jit(solution)/shard_map/while/body/eval_jaxpr/transpose(jvp())/dot_general | solution.py:14
  141.0 0.5 copy.25
  141.5 1.2 concatenate.17
  142.7 0.2 concatenate.18
  142.9 0.1 pad_maximum_fusion
  143.0 0.4 copy.29
  143.4 2.2 reduce.5
  145.7 0.2 reshape.184
  145.8 14.9 %all_to_all.26 = bf16[8,2,8192]{2,1,0:T(2,128)(2,1)S(1)} all-to-all(bf16[8,2,8192]{2,1,0:T(2,128)(2,1)S(1)} %reshape.184), channel_id=1, replica_groups=mesh['head'=8,'client'=4] {'head'}, dimensions={0} | all-to-all | bytes 524288 | tf_op jit(solution)/shard_map/all_to_all | solution.py:84
  160.7 0.3 reshape.185
  161.0 1.0 copy.27
  162.0 0.0 all-gather.13.cloned.1.call-start
  162.1 14.9 %all-gather.11.cloned.1.call-done = bf16[1,32,16384]{2,1,0:T(8,128)(2,1)} async-done(((bf16[1,8,16384]{2,1,0:T(8,128)(2,1)}), bf16[1,32,16384]{2,1,0:T(8,128)(2,1)}) %all-gather.11.cloned.1.call-update) | async-done | bytes 1048592 | tf_op jit(solution)/shard_map/all_gather | solution.py:85
  177.0 16.1 %fusion.30 = f32[32,1024]{1,0:T(8,128)} fusion(bf16[1024,16384]{1,0:T(8,128)(2,1)} %param.13, bf16[1,32,16384]{2,1,0:T(8,128)(2,1)} %all-gather.11.cloned.1.call-done), kind=kOutput, calls=%fused_computation.52 | convolution fusion | flops 1073741824 | bytes 34734080 | tf_op jit(solution)/shard_map/dot_general | solution.py:90
  193.6 14.9 %convolution_convert_fusion = bf16[1024,16384]{1,0:T(8,128)(2,1)} fusion(bf16[1,32,16384]{2,1,0:T(8,128)(2,1)S(1)} %copy-done.6, f32[32,1024]{1,0:T(8,128)S(1)} %convolution_add_fusion), kind=kOutput, calls=%fused_computation.1 | convolution fusion | flops 1090584576 | bytes 34734080 | tf_op jit(solution)/shard_map/dot_general | solution.py:87
  208.5 24.9 %all-gather.13.cloned.1.call-done = f32[256,1024]{1,0:T(8,128)} async-done(((f32[32,1024]{1,0:T(8,128)}), f32[256,1024]{1,0:T(8,128)}) %all-gather.13.cloned.1.call-update) | async-done | bytes 1048592 | tf_op jit(solution)/shard_map/all_gather | solution.py:95
  233.5 1.3 reduce_sum.120
  234.8 1.6 fusion.42
  (28 shorter events, 0.2 us)
Async XLA Ops:
  7.2 2.5 %copy-start = (bf16[256,1024]{1,0:T(8,128)(2,1)S(1)}, bf16[256,1024]{1,0:T(8,128)(2,1)}, u32[]{:S(2)}) copy-start(bf16[256,1024]{1,0:T(8,128)(2,1)} %param.11) | copy-start | bytes 1572868
  7.2 52.3 %reduce-scatter.2.cloned.1.call-start = ((), (), s32[]{:S(2)}) async-start(), calls=%async_computation.3 | async-start | bytes 2621440 | tf_op jit(solution)/shard_map/reduce_scatter | solution.py:70
  25.4 58.2 %copy-start.7 = (s32[1,256]{1,0:T(1,128)S(1)}, s32[1,256]{1,0:T(1,128)}, u32[]{:S(2)}) copy-start(s32[1,256]{1,0:T(1,128)} %param.14) | copy-start | bytes 3076
  25.4 58.2 %all-gather.7.cloned.1.call-start = ((), (), s32[]{:S(2)}) async-start(), calls=%async_computation.4 | async-start | bytes 2621440 | tf_op jit(solution)/shard_map/all_gather | solution.py:62
  26.2 81.6 %all-gather.9.cloned.1.call-start = ((), (), s32[]{:S(2)}) async-start(), calls=%async_computation.5 | async-start | bytes 2621440 | tf_op jit(solution)/shard_map/all_gather | solution.py:63
  62.8 25.2 %all-to-all-start = ((bf16[8,2,8192]{2,1,0:T(2,128)(2,1)}), bf16[8,2,8192]{2,1,0:T(2,128)(2,1)S(1)}, u32[]{:S(2)}, u32[]{:S(2)}) async-start(bf16[8,2,8192]{2,1,0:T(2,128)(2,1)} %reshape.182), calls=%async_computation.1 | async-start | bytes 524288 | tf_op jit(solution)/shard_map/all_to_all | solution.py:76
  68.3 108.7 %all-gather.11.cloned.1.call-start = ((), (), s32[]{:S(2)}) async-start(), calls=%async_computation.6 | async-start | bytes 1310720 | tf_op jit(solution)/shard_map/all_gather | solution.py:85
  91.2 5.1 %copy-start.2 = (f32[256,4096]{1,0:T(8,128)S(1)}, f32[256,4096]{1,0:T(8,128)}, u32[]{:S(2)}) copy-start(f32[256,4096]{1,0:T(8,128)} %get-tuple-element.34) | copy-start | bytes 12582916
  100.6 11.1 %copy-start.8 = (s32[1,256]{1,0:T(1,128)S(1)}, s32[1,256]{1,0:T(1,128)}, u32[]{:S(2)}) copy-start(s32[1,256]{1,0:T(1,128)} %param.15) | copy-start | bytes 3076
  107.8 4.6 %copy-start.4 = (f32[256,4096]{1,0:T(8,128)S(1)}, f32[256,4096]{1,0:T(8,128)}, u32[]{:S(2)}) copy-start(f32[256,4096]{1,0:T(8,128)} %get-tuple-element.36) | copy-start | bytes 12582916
  107.8 4.7 %copy-start.5 = (bf16[256,4096]{1,0:T(8,128)(2,1)S(1)}, bf16[256,4096]{1,0:T(8,128)(2,1)}, u32[]{:S(2)}) copy-start(bf16[256,4096]{1,0:T(8,128)(2,1)} %all-gather.9.cloned.1.call-done) | copy-start | bytes 6291460
  116.3 3.1 %copy-start.3 = (f32[256,4096]{1,0:T(8,128)S(1)}, f32[256,4096]{1,0:T(8,128)}, u32[]{:S(2)}) copy-start(f32[256,4096]{1,0:T(8,128)} %get-tuple-element.34) | copy-start | bytes 12582916
  162.0 71.4 %all-gather.13.cloned.1.call-start = ((), (), s32[]{:S(2)}) async-start(), calls=%async_computation.7 | async-start | bytes 1179648 | tf_op jit(solution)/shard_map/all_gather | solution.py:95
  177.0 16.7 %copy-start.6 = (bf16[1,32,16384]{2,1,0:T(8,128)(2,1)S(1)}, bf16[1,32,16384]{2,1,0:T(8,128)(2,1)}, u32[]{:S(2)}) copy-start(bf16[1,32,16384]{2,1,0:T(8,128)(2,1)} %all-gather.11.cloned.1.call-done) | copy-start | bytes 3145732
  193.6 42.7 %copy-start.1 = (bf16[256,1024]{1,0:T(8,128)(2,1)S(1)}, bf16[256,1024]{1,0:T(8,128)(2,1)}, u32[]{:S(2)}) copy-start(bf16[256,1024]{1,0:T(8,128)(2,1)} %param.11) | copy-start | bytes 1572868
Sparse Core Ops, SparseCore 0:
  25.6 33.9 reduce-scatter.1
  61.1 22.5 all-gather.6
  85.2 22.5 all-gather.8
  162.1 14.7 all-gather.10
  193.2 40.2 all-gather.12
